TPU v7x, 32 devices: a whole 2x2x4 slice. The times are simulated.
32 devices in a mesh: grp: 2 (over x), shard: 16 (over z, y, core).
Axes of the slice: x: 2, y: 2, z: 4, core: 2. Of those that a mesh axis runs over, the one named last changes fastest.
Arguments:
- window: bfloat16 [32, 4096], P('grp'), may hold values from -6 to 6
- weight: bfloat16 [11008, 4096], P('shard'), may hold values from -0.09375 to 0.09375
- factor_a: bfloat16 [64, 4, 4096], P(('grp', 'shard')), may hold values from -6 to 6
- factor_b: bfloat16 [64, 4, 11008], P(('grp', 'shard')), may hold values from -6 to 6
- fitness: float32 [64], P(('grp', 'shard')), may hold values from -4 to 4
Outputs:
- perturbed: bfloat16 [11008, 1024], P('shard', 'grp')
- update: float32 [11008, 4096], P('shard', 'grp')
All inputs are finite; a program needn't handle non-finite values.
Results may differ from a plain program's by a relative error of at most 0.0029.
Values may be sent and summed in bfloat16 or wider, within the bound.
A program may use at most 64 MiB of HBM per device.

v0:
```python
import math
import jax
import jax.numpy as jnp
from jax import lax
from jax.sharding import PartitionSpec as P


def contract(left_rows, right_rows):
    return lax.dot_general(
        left_rows, right_rows, (((0,), (0,)), ((), ())), preferred_element_type=jnp.float32
    )


def local(window, weight, factor_a, factor_b, fitness):
    model_width = window.shape[1]
    cand_dev, factor_rank, _ = factor_a.shape
    shard_count = lax.axis_size("shard")
    total_cands = cand_dev * lax.axis_size("grp") * shard_count
    perturb = 0.25 / math.sqrt(model_width)
    step_scale = 0.5 / math.sqrt(total_cands)
    base_out = lax.dot_general(
        weight, window, (((1,), (1,)), ((), ())), preferred_element_type=jnp.float32
    )
    projected = jnp.einsum("td,crd->crt", window, factor_a, preferred_element_type=jnp.float32)
    projected_all, fitness_all = (
        lax.all_gather(projected, "shard", axis=0, tiled=True),
        lax.all_gather(fitness, "shard", axis=0, tiled=True),
    )
    columns = lax.all_to_all(factor_b, "shard", split_axis=2, concat_axis=0, tiled=True)
    col_width = columns.shape[2]
    low_rank = jnp.einsum(
        "crt,crf->fct", projected_all, columns.astype(jnp.float32), precision=lax.Precision.HIGHEST
    )
    perturbed = (
        (base_out[:, None, :] + perturb * low_rank).astype(jnp.bfloat16).reshape(col_width, -1)
    )
    weighted = (fitness_all[:, None, None] * columns.astype(jnp.float32)).astype(jnp.bfloat16)
    exchanged = lax.all_to_all(factor_a, "grp", split_axis=2, concat_axis=0, tiled=True)
    weighted_four = weighted.reshape(shard_count, cand_dev, factor_rank, col_width)
    weighted_flat = lax.all_gather(weighted_four, "grp", axis=1, tiled=True).reshape(-1, col_width)
    owned_width = exchanged.shape[2]
    block_width = owned_width // 4
    update_parts = []
    for part_index in range(4):
        factor_slab = exchanged[:, :, part_index * block_width : (part_index + 1) * block_width]
        gathered = lax.all_gather(factor_slab, "shard", axis=0, tiled=True)
        update_parts.append(contract(weighted_flat, gathered.reshape(-1, block_width)))
    update = jnp.concatenate(update_parts, 1) * step_scale
    return (perturbed, update)


def solution(mesh):
    in_specs = (
        P("grp", None),
        P("shard", None),
        P(("grp", "shard"), None, None),
        P(("grp", "shard"), None, None),
        P(("grp", "shard")),
    )
    out_specs = (P("shard", "grp"), P("shard", "grp"))
    return jax.shard_map(local, mesh=mesh, in_specs=in_specs, out_specs=out_specs, check_vma=False)
```

profile of v0, /device:TPU:0, one launch (start us, length us, event | category | flops | bytes accessed | tf_op | source)
XLA Modules:
  0.0 226.9 jit_solution(7585882269689568177)
XLA Ops:
  0.6 4.4 %copy.14 = bf16[2,4,4096]{1,0,2:T(2,128)(2,1)S(1)} copy(bf16[2,4,4096]{2,1,0:T(4,128)(2,1)} %param.7) | data formatting | bytes 131072 | tf_op args[2]
  5.1 4.6 %reshape.41 = bf16[2,2,8192]{2,1,0:T(2,128)(2,1)} reshape(bf16[4096,2,4]{2,1,0:T(2,128)(2,1)S(1)} %bitcast.38) | data formatting | bytes 131072
  9.7 4.2 %all-to-all-start.1 = ((bf16[2,2,8192]{2,1,0:T(2,128)(2,1)}), bf16[2,2,8192]{2,1,0:T(2,128)(2,1)S(1)}, u32[]{:S(2)}, u32[]{:S(2)}) async-start(bf16[2,2,8192]{2,1,0:T(2,128)(2,1)} %reshape.41), calls=%async_computation.1 | async-start | bytes 131072 | tf_op jit(solution)/shard_map/all_to_all | solution.py:38
  13.9 4.8 %fusion.4 = f32[688,16]{0,1:T(8,128)} fusion(bf16[688,4096]{1,0:T(8,128)(2,1)} %param.6, bf16[16,4096]{1,0:T(8,128)(2,1)S(1)} %copy-done), kind=kOutput, calls=%fused_computation.7 | convolution fusion | flops 90177536 | bytes 5811200 | tf_op jit(solution)/shard_map/dot_general | solution.py:21
  18.7 0.2 fusion.1
  19.0 9.0 %copy.12 = bf16[2,4,11008]{1,0,2:T(2,128)(2,1)} copy(bf16[2,4,11008]{2,1,0:T(4,128)(2,1)S(1)} %copy-done.3) | data formatting | bytes 352256 | tf_op args[3]
  28.0 15.1 %reshape.39 = bf16[16,2,2752]{2,1,0:T(2,128)(2,1)} reshape(bf16[11008,2,4]{2,1,0:T(2,128)(2,1)} %bitcast.36) | data formatting | bytes 352256
  43.0 0.6 dynamic-slice
  44.3 0.2 dynamic-update-slice
  44.5 34.0 %all-reduce = f32[32]{0:T(128)S(1)} all-reduce(f32[32]{0:T(128)S(1)} %dynamic-update-slice), channel_id=1, replica_groups=mesh['grp'=2,'shard'=16] {'shard'}, use_global_device_ids=true, to_apply=%add | all-reduce | flops 32 | bytes 256
  78.7 18.7 %all_gather.21 = f32[32,4,16]{2,1,0:T(4,128)} all-gather(f32[2,4,16]{2,1,0:T(4,128)S(1)} %fusion.1), channel_id=1, replica_groups=mesh['grp'=2,'shard'=16] {'shard'}, dimensions={0}, use_global_device_ids=true | all-gather | bytes 8704 | tf_op jit(solution)/shard_map/all_gather | solution.py:26
  97.4 3.5 %all-to-all-start = ((bf16[16,2,2752]{2,1,0:T(2,128)(2,1)}), bf16[16,2,2752]{2,1,0:T(2,128)(2,1)S(1)}, u32[]{:S(2)}, u32[]{:S(2)}) async-start(bf16[16,2,2752]{2,1,0:T(2,128)(2,1)} %reshape.39), calls=%async_computation | async-start | bytes 360448 | tf_op jit(solution)/shard_map/all_to_all | solution.py:29
  100.9 4.5 %reshape.42 = bf16[4096,2,4]{2,1,0:T(2,128)(2,1)S(1)} reshape(bf16[2,2,8192]{2,1,0:T(2,128)(2,1)S(1)} %all-to-all-done.1) | data formatting | bytes 131072
  105.4 1.4 copy.15
  106.9 22.4 %all_gather.24 = bf16[64,4,512]{2,1,0:T(4,128)(2,1)S(1)} all-gather(bf16[4,4,512]{2,1,0:T(4,128)(2,1)S(1)} %get-tuple-element.8), channel_id=1, replica_groups=mesh['grp'=2,'shard'=16] {'shard'}, dimensions={0}, use_global_device_ids=true | all-gather | bytes 278528 | tf_op jit(solution)/shard_map/all_gather | solution.py:46
  129.3 18.2 %all_gather.25 = bf16[64,4,512]{2,1,0:T(4,128)(2,1)S(1)} all-gather(bf16[4,4,512]{2,1,0:T(4,128)(2,1)S(1)} %get-tuple-element.11), channel_id=1, replica_groups=mesh['grp'=2,'shard'=16] {'shard'}, dimensions={0}, use_global_device_ids=true | all-gather | bytes 278528 | tf_op jit(solution)/shard_map/all_gather | solution.py:46
  147.5 0.8 reshape.30
  148.2 19.5 %all_gather.26 = bf16[64,4,512]{2,1,0:T(4,128)(2,1)S(1)} all-gather(bf16[4,4,512]{2,1,0:T(4,128)(2,1)S(1)} %get-tuple-element.10), channel_id=1, replica_groups=mesh['grp'=2,'shard'=16] {'shard'}, dimensions={0}, use_global_device_ids=true | all-gather | bytes 278528 | tf_op jit(solution)/shard_map/all_gather | solution.py:46
  167.7 0.8 reshape.31
  168.5 18.1 %all_gather.27 = bf16[64,4,512]{2,1,0:T(4,128)(2,1)S(1)} all-gather(bf16[4,4,512]{2,1,0:T(4,128)(2,1)S(1)} %get-tuple-element.9), channel_id=1, replica_groups=mesh['grp'=2,'shard'=16] {'shard'}, dimensions={0}, use_global_device_ids=true | all-gather | bytes 278528 | tf_op jit(solution)/shard_map/all_gather | solution.py:46
  186.6 0.8 reshape.32
  187.4 7.4 %reshape.40 = bf16[11008,2,4]{2,1,0:T(2,128)(2,1)} reshape(bf16[16,2,2752]{2,1,0:T(2,128)(2,1)S(1)} %all-to-all-done) | data formatting | bytes 352256
  194.8 10.7 %copy.13 = bf16[2,4,16,688]{3,1,0,2:T(4,128)(2,1)S(1)} copy(bf16[2,4,16,688]{1,0,3,2:T(2,128)(2,1)} %bitcast.35) | data formatting | bytes 352256 | tf_op jit(solution)/shard_map/all_to_all | solution.py:29
  205.6 8.0 %all_gather.23 = bf16[16,4,4,688]{3,2,1,0:T(4,128)(2,1)S(1)} all-gather(bf16[16,2,4,688]{3,2,1,0:T(4,128)(2,1)S(1)} %multiply_convert_fusion), channel_id=1, replica_groups=mesh['grp'=2,'shard'=16] {'grp'}, dimensions={1}, use_global_device_ids=true | all-gather | bytes 528384 | tf_op jit(solution)/shard_map/all_gather | solution.py:40
  213.6 0.2 reshape.28
  213.8 0.4 fusion.5
  214.2 1.4 fusion.6
  215.6 1.5 fusion.7
  217.1 1.5 fusion.8
  218.5 1.8 fusion
  220.3 2.2 copy.16
  222.6 4.4 %maximum_multiply_fusion = f32[688,2048]{1,0:T(8,128)} fusion(f32[688,512]{1,0:T(8,128)} %fusion.8, f32[688,512]{1,0:T(8,128)} %fusion.7, f32[688,512]{1,0:T(8,128)S(1)} %fusion.6, f32[688,512]{1,0:T(8,128)S(1)} %fusion.5), kind=kLoop, calls=%fused_computation | loop fusion | flops 5636096 | bytes 11272192 | tf_op jit(solution)/shard_map/mul | solution.py:48
  (25 shorter events, 0.4 us)
Async XLA Ops:
  0.6 13.3 %copy-start = (bf16[16,4096]{1,0:T(8,128)(2,1)S(1)}, bf16[16,4096]{1,0:T(8,128)(2,1)}, u32[]{:S(2)}) copy-start(bf16[16,4096]{1,0:T(8,128)(2,1)} %param.5) | copy-start | bytes 393220
  9.7 87.7 %all-to-all-start.1 = ((bf16[2,2,8192]{2,1,0:T(2,128)(2,1)}), bf16[2,2,8192]{2,1,0:T(2,128)(2,1)S(1)}, u32[]{:S(2)}, u32[]{:S(2)}) async-start(bf16[2,2,8192]{2,1,0:T(2,128)(2,1)} %reshape.41), calls=%async_computation.1 | async-start | bytes 131072 | tf_op jit(solution)/shard_map/all_to_all | solution.py:38
  13.9 4.8 %copy-start.4 = (bf16[2,4,4096]{2,1,0:T(4,128)(2,1)S(1)}, bf16[2,4,4096]{2,1,0:T(4,128)(2,1)}, u32[]{:S(2)}) copy-start(bf16[2,4,4096]{2,1,0:T(4,128)(2,1)} %param.7) | copy-start | bytes 196612
  13.9 5.1 %copy-start.3 = (bf16[2,4,11008]{2,1,0:T(4,128)(2,1)S(1)}, bf16[2,4,11008]{2,1,0:T(4,128)(2,1)}, u32[]{:S(2)}) copy-start(bf16[2,4,11008]{2,1,0:T(4,128)(2,1)} %param.8) | copy-start | bytes 528388
  28.0 15.1 %copy-start.8 = (u32[32]{0:T(128)S(1)}, u32[32]{0:T(128)}, u32[]{:S(2)}) copy-start(u32[32]{0:T(128)} %constant.9) | copy-start | bytes 388
  28.0 16.3 %copy-start.7 = (f32[2]{0:T(128)S(1)}, f32[2]{0:T(128)}, u32[]{:S(2)}) copy-start(f32[2]{0:T(128)} %param.9) | copy-start | bytes 28
  97.4 90.0 %all-to-all-start = ((bf16[16,2,2752]{2,1,0:T(2,128)(2,1)}), bf16[16,2,2752]{2,1,0:T(2,128)(2,1)S(1)}, u32[]{:S(2)}, u32[]{:S(2)}) async-start(bf16[16,2,2752]{2,1,0:T(2,128)(2,1)} %reshape.39), calls=%async_computation | async-start | bytes 360448 | tf_op jit(solution)/shard_map/all_to_all | solution.py:29
  213.8 1.8 copy-start.1
  214.2 2.9 %copy-start.2 = (bf16[256,512]{1,0:T(8,128)(2,1)S(1)}, bf16[256,512]{1,0:T(8,128)(2,1)}, u32[]{:S(2)}) copy-start(bf16[256,512]{1,0:T(8,128)(2,1)} %reshape.32) | copy-start | bytes 786436
  215.6 3.0 %copy-start.5 = (f32[32,4,16]{2,1,0:T(4,128)S(1)}, f32[32,4,16]{2,1,0:T(4,128)}, u32[]{:S(2)}) copy-start(f32[32,4,16]{2,1,0:T(4,128)} %all_gather.21) | copy-start | bytes 24580
  215.6 3.0 %copy-start.6 = (f32[688,16]{0,1:T(8,128)S(1)}, f32[688,16]{0,1:T(8,128)}, u32[]{:S(2)}) copy-start(f32[688,16]{0,1:T(8,128)} %fusion.4) | copy-start | bytes 132100
where the time goes:
time: 228 us; the launch traced here: 227 us
  blocking collectives  139 us (61%)
  local copies, waits for them, and re-layouts  62.9 us (28%)
  matrix products  11.5 us (5%)
  starting transfers between devices  7.75 us (3%)
  other arithmetic  4.51 us (2%)
    all_gather x4, blocking collectives, local(): gathered = lax.all_gather(factor_slab, 'shard', axis=0, tiled=True)  78.1 us
    unnamed x28, local copies, waits for them, and re-layouts  48.1 us
    unnamed x1, blocking collectives  34 us
    all_gather x1, blocking collectives, local(): lax.all_gather(projected, 'shard', axis=0, tiled=True)  18.7 us
    all_to_all x1, local copies, waits for them, and re-layouts, local(): lax.all_to_all(factor_b, 'shard', split_axis=2, concat_axis=0, tiled=True)  10.7 us
    all_gather x1, blocking collectives, local(): lax.all_gather(weighted_four, 'grp', axis=1, tiled=True)  8 us
    dot_general x1, matrix products, local(): lax.dot_general(weight, window, (((1,), (1,)), ((), ())), preferred_eleme...  4.83 us
    dot_general x4, matrix products, contract(): lax.dot_general(left_rows, right_rows, (((0,), (0,)), ((), ())), preferre...  4.67 us
  transfers between devices with their start and end apart: 2, of which 0 were waited for; matrix products, arithmetic and copies ran while one was open for 17% of the time, Pallas kernels for 0%

commit v1 on v0

--- a/solution.py
+++ b/solution.py
@@ -3,6 +3,13 @@
 import jax.numpy as jnp
 from jax import lax
 from jax.sharding import PartitionSpec as P
+
+
+def swap_blocks(block, axis, split, join):
+    size = lax.axis_size(axis)
+    blocks = jnp.stack(jnp.split(block, size, axis=split), axis=0)
+    blocks = lax.all_to_all(blocks, axis, split_axis=0, concat_axis=0)
+    return jnp.concatenate(blocks, axis=join)
 
 
 def contract(left_rows, right_rows):
@@ -26,7 +33,7 @@
         lax.all_gather(projected, "shard", axis=0, tiled=True),
         lax.all_gather(fitness, "shard", axis=0, tiled=True),
     )
-    columns = lax.all_to_all(factor_b, "shard", split_axis=2, concat_axis=0, tiled=True)
+    columns = swap_blocks(factor_b, "shard", 2, 0)
     col_width = columns.shape[2]
     low_rank = jnp.einsum(
         "crt,crf->fct", projected_all, columns.astype(jnp.float32), precision=lax.Precision.HIGHEST

time: 228 us -> 195 us (0.86)
  local copies, waits for them, and re-layouts: 62.9 us -> 32 us
    unnamed x28 -> x42, local copies, waits for them, and re-layouts: 48.1 us -> 27.2 us
    all_to_all x1 -> x0, local copies, waits for them, and re-layouts: 10.7 us -> none  [local(): lax.all_to_all(factor_b, 'shard', split_axis=2, concat_axis=0, tiled=True)]
  transfers between devices with their start and end apart: 2 -> 2, of which waited for: 0 -> 0; matrix products, arithmetic and copies ran while one was open for 17% -> 13% of each run, Pallas kernels for 0% -> 0%
where the time goes in v1:
time: 195 us
  blocking collectives  139 us (71%)
  local copies, waits for them, and re-layouts  32 us (16%)
  matrix products  10.5 us (5%)
  starting transfers between devices  7.76 us (4%)
  other arithmetic  4.49 us (2%)
    all_gather x4, blocking collectives, local(): gathered = lax.all_gather(factor_slab, 'shard', axis=0, tiled=True)  78.1 us
    unnamed x1, blocking collectives  34 us
    unnamed x42, local copies, waits for them, and re-layouts  27.2 us
    all_gather x1, blocking collectives, local(): lax.all_gather(projected, 'shard', axis=0, tiled=True)  18.7 us
    all_gather x1, blocking collectives, local(): lax.all_gather(weighted_four, 'grp', axis=1, tiled=True)  7.82 us
    dot_general x1, matrix products, local(): lax.dot_general(weight, window, (((1,), (1,)), ((), ())), preferred_eleme...  4.83 us
    mul x1, other arithmetic, local(): update = jnp.concatenate(update_parts, 1) * step_scale  4.35 us
    all_to_all x1, starting transfers between devices, local(): lax.all_to_all(factor_a, 'grp', split_axis=2, concat_axis=0, tiled=True)  4.23 us
  transfers between devices with their start and end apart: 2, of which 0 were waited for; matrix products, arithmetic and copies ran while one was open for 13% of the time, Pallas kernels for 0%

profile of v1, /device:TPU:0, one launch (start us, length us, event | category | flops | bytes accessed | tf_op | source)
XLA Modules:
  0.0 194.8 jit_solution(16529497137692406822)
XLA Ops:
  0.6 4.4 %copy.10 = bf16[2,4,4096]{1,0,2:T(2,128)(2,1)S(1)} copy(bf16[2,4,4096]{2,1,0:T(4,128)(2,1)} %param.7) | data formatting | bytes 131072 | tf_op args[2]
  5.1 4.6 %reshape.43 = bf16[2,2,8192]{2,1,0:T(2,128)(2,1)} reshape(bf16[4096,2,4]{2,1,0:T(2,128)(2,1)S(1)} %bitcast.60) | data formatting | bytes 131072
  9.7 4.2 %all-to-all-start.1 = ((bf16[2,2,8192]{2,1,0:T(2,128)(2,1)}), bf16[2,2,8192]{2,1,0:T(2,128)(2,1)S(1)}, u32[]{:S(2)}, u32[]{:S(2)}) async-start(bf16[2,2,8192]{2,1,0:T(2,128)(2,1)} %reshape.43), calls=%async_computation.1 | async-start | bytes 131072 | tf_op jit(solution)/shard_map/all_to_all | solution.py:45
  14.5 0.7 constant_dynamic-update-slice_fusion.14
  15.9 0.7 constant_dynamic-update-slice_fusion.12
  16.6 0.7 constant_dynamic-update-slice_fusion.11
  17.9 0.7 constant_dynamic-update-slice_fusion.9
  18.6 0.7 constant_dynamic-update-slice_fusion.8
  19.9 0.7 constant_dynamic-update-slice_fusion.6
  21.2 0.7 constant_dynamic-update-slice_fusion.4
  21.9 0.7 constant_dynamic-update-slice_fusion.3
  22.6 0.7 constant_dynamic-update-slice_fusion.2
  24.2 4.8 %fusion.3 = f32[688,16]{0,1:T(8,128)} fusion(bf16[688,4096]{1,0:T(8,128)(2,1)} %param.6, bf16[16,4096]{1,0:T(8,128)(2,1)S(1)} %copy-done), kind=kOutput, calls=%fused_computation.22 | convolution fusion | flops 90177536 | bytes 5811200 | tf_op jit(solution)/shard_map/dot_general | solution.py:28
  29.0 0.7 constant_dynamic-update-slice_fusion
  31.2 34.0 %all-reduce = f32[32]{0:T(128)S(1)} all-reduce(f32[32]{0:T(128)S(1)} %dynamic-update-slice), channel_id=1, replica_groups=mesh['grp'=2,'shard'=16] {'shard'}, use_global_device_ids=true, to_apply=%add | all-reduce | flops 32 | bytes 256
  65.3 18.7 %all_gather.21 = f32[32,4,16]{2,1,0:T(4,128)} all-gather(f32[2,4,16]{2,1,0:T(4,128)S(1)} %fusion), channel_id=1, replica_groups=mesh['grp'=2,'shard'=16] {'shard'}, dimensions={0}, use_global_device_ids=true | all-gather | bytes 8704 | tf_op jit(solution)/shard_map/all_gather | solution.py:33
  84.0 3.5 %all-to-all-start = ((bf16[16,2,4,688]{3,2,1,0:T(4,128)(2,1)}), bf16[16,2,4,688]{3,2,1,0:T(4,128)(2,1)S(1)}, u32[]{:S(2)}, u32[]{:S(2)}) async-start(bf16[16,2,4,688]{3,2,1,0:T(4,128)(2,1)} %constant_dynamic-update-slice_fusion), calls=%async_computation | async-start | bytes 393216 | tf_op jit(solution)/shard_map/all_to_all | solution.py:11
  87.5 4.5 %reshape.44 = bf16[4096,2,4]{2,1,0:T(2,128)(2,1)S(1)} reshape(bf16[2,2,8192]{2,1,0:T(2,128)(2,1)S(1)} %all-to-all-done.1) | data formatting | bytes 131072
  92.0 1.4 copy.11
  93.5 22.4 %all_gather.24 = bf16[64,4,512]{2,1,0:T(4,128)(2,1)S(1)} all-gather(bf16[4,4,512]{2,1,0:T(4,128)(2,1)S(1)} %get-tuple-element.8), channel_id=1, replica_groups=mesh['grp'=2,'shard'=16] {'shard'}, dimensions={0}, use_global_device_ids=true | all-gather | bytes 278528 | tf_op jit(solution)/shard_map/all_gather | solution.py:53
  115.9 18.2 %all_gather.25 = bf16[64,4,512]{2,1,0:T(4,128)(2,1)S(1)} all-gather(bf16[4,4,512]{2,1,0:T(4,128)(2,1)S(1)} %get-tuple-element.11), channel_id=1, replica_groups=mesh['grp'=2,'shard'=16] {'shard'}, dimensions={0}, use_global_device_ids=true | all-gather | bytes 278528 | tf_op jit(solution)/shard_map/all_gather | solution.py:53
  134.1 0.8 reshape.34
  134.9 19.5 %all_gather.26 = bf16[64,4,512]{2,1,0:T(4,128)(2,1)S(1)} all-gather(bf16[4,4,512]{2,1,0:T(4,128)(2,1)S(1)} %get-tuple-element.10), channel_id=1, replica_groups=mesh['grp'=2,'shard'=16] {'shard'}, dimensions={0}, use_global_device_ids=true | all-gather | bytes 278528 | tf_op jit(solution)/shard_map/all_gather | solution.py:53
  154.3 0.8 reshape.35
  155.1 18.1 %all_gather.27 = bf16[64,4,512]{2,1,0:T(4,128)(2,1)S(1)} all-gather(bf16[4,4,512]{2,1,0:T(4,128)(2,1)S(1)} %get-tuple-element.9), channel_id=1, replica_groups=mesh['grp'=2,'shard'=16] {'shard'}, dimensions={0}, use_global_device_ids=true | all-gather | bytes 278528 | tf_op jit(solution)/shard_map/all_gather | solution.py:53
  173.2 0.8 reshape.36
  174.1 7.8 %all_gather.23 = bf16[16,4,4,688]{3,2,1,0:T(4,128)(2,1)S(1)} all-gather(bf16[16,2,4,688]{3,2,1,0:T(4,128)(2,1)S(1)} %multiply_convert_fusion), channel_id=1, replica_groups=mesh['grp'=2,'shard'=16] {'grp'}, dimensions={1}, use_global_device_ids=true | all-gather | bytes 528384 | tf_op jit(solution)/shard_map/all_gather | solution.py:47
  183.5 1.5 fusion.6
  185.0 1.5 fusion.7
  186.5 1.7 add_convert_fusion
  188.2 2.2 %copy.12 = bf16[688,512]{1,0:T(8,128)(2,1)} copy(bf16[688,512]{0,1:T(8,128)(2,1)} %bitcast.61) | data formatting | bytes 1409024
  190.4 4.4 %maximum_multiply_fusion = f32[688,2048]{1,0:T(8,128)} fusion(f32[688,512]{1,0:T(8,128)} %fusion.7, f32[688,512]{1,0:T(8,128)} %fusion.6, f32[688,512]{1,0:T(8,128)S(1)} %fusion.5, f32[688,512]{1,0:T(8,128)S(1)} %fusion.4), kind=kLoop, calls=%fused_computation | loop fusion | flops 5636096 | bytes 11272192 | tf_op jit(solution)/shard_map/mul | solution.py:55
  (39 shorter events, 6.8 us)
Async XLA Ops:
  0.6 23.3 %copy-start = (bf16[16,4096]{1,0:T(8,128)(2,1)S(1)}, bf16[16,4096]{1,0:T(8,128)(2,1)}, u32[]{:S(2)}) copy-start(bf16[16,4096]{1,0:T(8,128)(2,1)} %param.5) | copy-start | bytes 393220
  5.1 8.9 %copy-start.4 = (bf16[2,4,11008]{2,1,0:T(4,128)(2,1)S(1)}, bf16[2,4,11008]{2,1,0:T(4,128)(2,1)}, u32[]{:S(2)}) copy-start(bf16[2,4,11008]{2,1,0:T(4,128)(2,1)} %param.8) | copy-start | bytes 528388
  5.1 18.9 %copy-start.5 = (bf16[2,4,4096]{2,1,0:T(4,128)(2,1)S(1)}, bf16[2,4,4096]{2,1,0:T(4,128)(2,1)}, u32[]{:S(2)}) copy-start(bf16[2,4,4096]{2,1,0:T(4,128)(2,1)} %param.7) | copy-start | bytes 196612
  9.7 74.3 %all-to-all-start.1 = ((bf16[2,2,8192]{2,1,0:T(2,128)(2,1)}), bf16[2,2,8192]{2,1,0:T(2,128)(2,1)S(1)}, u32[]{:S(2)}, u32[]{:S(2)}) async-start(bf16[2,2,8192]{2,1,0:T(2,128)(2,1)} %reshape.43), calls=%async_computation.1 | async-start | bytes 131072 | tf_op jit(solution)/shard_map/all_to_all | solution.py:45
  24.2 5.5 %copy-start.9 = (u32[32]{0:T(128)S(1)}, u32[32]{0:T(128)}, u32[]{:S(2)}) copy-start(u32[32]{0:T(128)} %constant.9) | copy-start | bytes 388
  24.2 6.8 %copy-start.8 = (f32[2]{0:T(128)S(1)}, f32[2]{0:T(128)}, u32[]{:S(2)}) copy-start(f32[2]{0:T(128)} %param.9) | copy-start | bytes 28
  84.0 90.0 %all-to-all-start = ((bf16[16,2,4,688]{3,2,1,0:T(4,128)(2,1)}), bf16[16,2,4,688]{3,2,1,0:T(4,128)(2,1)S(1)}, u32[]{:S(2)}, u32[]{:S(2)}) async-start(bf16[16,2,4,688]{3,2,1,0:T(4,128)(2,1)} %constant_dynamic-update-slice_fusion), calls=%async_computation | async-start | bytes 393216 | tf_op jit(solution)/shard_map/all_to_all | solution.py:11
  182.1 1.0 copy-start.1
  182.1 1.3 copy-start.2
  183.1 1.9 copy-start.3
  183.5 3.0 %copy-start.6 = (f32[32,4,16]{2,1,0:T(4,128)S(1)}, f32[32,4,16]{2,1,0:T(4,128)}, u32[]{:S(2)}) copy-start(f32[32,4,16]{2,1,0:T(4,128)} %all_gather.21) | copy-start | bytes 24580
  183.5 3.0 %copy-start.7 = (f32[688,16]{0,1:T(8,128)S(1)}, f32[688,16]{0,1:T(8,128)}, u32[]{:S(2)}) copy-start(f32[688,16]{0,1:T(8,128)} %fusion.3) | copy-start | bytes 132100
